TPU v7x, 32 devices: a whole 2x2x4 slice. The times are simulated.
32 devices in a mesh: rep: 2 (over y), seq: 4 (over z), head: 2 (over x), sub: 2 (over core).
Axes of the slice: x: 2, y: 2, z: 4, core: 2. Of those that a mesh axis runs over, the one named last changes fastest.
Arguments:
- queries: bfloat16 [8, 8192], P('rep', 'head'), parts along dimension 0, may hold values from -4.5 to 4.5
- key_cache: bfloat16 [1024, 128, 1024], P(('rep', 'seq', 'sub'), None, 'head'), parts along dimension 0, may hold values from -4.5 to 4.5
- value_cache: bfloat16 [1024, 128, 1024], P(('rep', 'seq', 'sub'), None, 'head'), parts along dimension 0, may hold values from -6 to 6
- seq_lengths: int32 [8], P('rep'), parts along dimension 0, may hold values from 513 to 32768, as said below
- slot_owner: int32 [1024], P(('rep', 'seq', 'sub')), parts along dimension 0, may hold values from 0 to 3, as said below
- slot_page: int32 [1024], P(('rep', 'seq', 'sub')), parts along dimension 0, may hold values from 0 to 255, as said below
- out_weight: bfloat16 [8192, 8192], P('head', ('seq', 'sub')), may hold values from -0.0625 to 0.0625
Outputs:
- projected: bfloat16 [8, 8192], P('rep', ('seq', 'sub')), parts along dimension 0
There are 2 independent parts, one for each index of `rep`. A program takes and returns all parts, laid end to end along the dimension named above; an argument that names none is the same for every part. Nothing has to cross between parts.
Inputs may be any that keep to these rules, and one draw needn't show every extreme that they name: `slot_owner`: every sequence holds 5 to 256 pages, and some sequence exactly 256; its pages are numbered 0 upward and each stands in exactly one cache page; every cache page is used; a sequence's pages occupy consecutive cache pages. slot_page[s] < ceil(seq_lengths[slot_owner[s]] / 128), and every page below that count is present. seq_lengths[b] lies in the last of its sequence's pages.
All inputs are finite; a program needn't handle non-finite values.
Results may differ from a plain program's by a relative error of at most 0.0055.
Values may be sent and summed in bfloat16 or wider, within the bound.
A program may use at most 64 MiB of HBM per device.

v0:
```python
import jax
import jax.numpy as jnp
from jax import lax
from jax.sharding import PartitionSpec as P

DH = 128
PAGE = 128
neg_fill = -1e30


def merged(part, axis, combine):
    gathered = jax.tree.map(lambda a: lax.all_gather(a, axis), part)

    def take(source):
        return jax.tree.map(lambda a: lax.dynamic_index_in_dim(a, source, 0, False), gathered)

    return lax.fori_loop(
        1, lax.axis_size(axis), lambda source, state: combine(state, take(source)), take(0)
    )


def spread(values, factor):
    row_count, col_count = factor.shape
    return (values.reshape(row_count, col_count, -1) * factor[:, :, None]).reshape(row_count, -1)


def merge_states(first, second):
    top_first, mass_first, out_first = first
    top_second, mass_second, out_second = second
    joined = jnp.maximum(top_first, top_second)
    scale_first = jnp.exp(top_first - joined)
    scale_second = jnp.exp(top_second - joined)
    mass_joined = mass_first * scale_first + mass_second * scale_second
    out_joined = spread(out_first, scale_first) + spread(out_second, scale_second)
    return (joined, mass_joined, out_joined)


def on_device(queries, key_cache, value_cache, seq_lengths, slot_owner, slot_page, out_weight):
    batch_rows = queries.shape[0]
    slot_count = key_cache.shape[0]
    groups_local = key_cache.shape[2] // DH
    per_group = queries.shape[1] // (groups_local * DH)
    picked = jnp.take(queries, slot_owner, axis=0).reshape(slot_count, groups_local, per_group, DH)
    key_tiles = key_cache.reshape(slot_count, PAGE, groups_local, DH)
    value_tiles = value_cache.reshape(slot_count, PAGE, groups_local, DH)
    scores = jnp.einsum("sgjd,stgd->sgjt", picked, key_tiles, preferred_element_type=jnp.float32)
    scores = scores * (1.0 / jnp.sqrt(jnp.float32(DH)))
    valid = jnp.clip(jnp.take(seq_lengths, slot_owner, axis=0) - slot_page * PAGE, 0, PAGE)
    positions = jnp.arange(PAGE, dtype=jnp.int32)
    live = (positions[None, :] < valid[:, None])[:, None, None, :]
    scores = jnp.where(live, scores, neg_fill)
    page_peak = jnp.max(scores, axis=-1)
    probs = jnp.exp(scores - page_peak[..., None]).astype(jnp.bfloat16)
    page_mass = jnp.sum(probs.astype(jnp.float32), axis=-1)
    page_out = jnp.einsum("sgjt,stgd->sgjd", probs, value_tiles, preferred_element_type=jnp.float32)
    owner_hits = slot_owner[None, :] == jnp.arange(batch_rows, dtype=jnp.int32)[:, None]
    seq_peak = jnp.max(jnp.where(owner_hits[:, :, None, None], page_peak[None], neg_fill), axis=1)
    factor = jnp.exp(page_peak - jnp.take(seq_peak, slot_owner, axis=0))
    hit_float = owner_hits.astype(jnp.float32)
    heads_local = groups_local * per_group
    seq_mass = jnp.dot(
        hit_float,
        (page_mass * factor).reshape(slot_count, heads_local),
        precision=lax.Precision.HIGHEST,
        preferred_element_type=jnp.float32,
    )
    seq_out = jnp.dot(
        hit_float,
        (page_out * factor[..., None]).reshape(slot_count, heads_local * DH),
        precision=lax.Precision.HIGHEST,
        preferred_element_type=jnp.float32,
    )
    seq_peak = seq_peak.reshape(batch_rows, heads_local)
    top_all, mass_all, out_all = merged((seq_peak, seq_mass, seq_out), ("seq", "sub"), merge_states)
    attention = spread(out_all, 1.0 / mass_all).astype(jnp.bfloat16)
    partial_out = jnp.dot(attention, out_weight, preferred_element_type=jnp.float32)
    return lax.psum(partial_out, "head").astype(jnp.bfloat16)


def solution(mesh):
    in_specs = (
        P("rep", "head"),
        P(("rep", "seq", "sub"), None, "head"),
        P(("rep", "seq", "sub"), None, "head"),
        P("rep"),
        P(("rep", "seq", "sub")),
        P(("rep", "seq", "sub")),
        P("head", ("seq", "sub")),
    )
    out_specs = P("rep", ("seq", "sub"))
    return jax.shard_map(
        on_device, mesh=mesh, in_specs=in_specs, out_specs=out_specs, check_vma=False
    )
```

profile of v0, /device:TPU:0, one launch (start us, length us, event | category | flops | bytes accessed | tf_op | source)
XLA Modules:
  0.0 78.8 jit_solution(3403634785775584727)
XLA Ops:
  0.0 0.0 copy-start
  0.0 0.0 copy-start.1
  0.0 1.5 %fusion.40 = (s32[1]{0:T(128)}, s32[1]{0:T(128)}, s32[1]{0:T(128)}, s32[1]{0:T(128)}) fusion(s32[4]{0:T(128)} %param.12), kind=kLoop, calls=%fused_computation.62 | loop fusion | bytes 32 | tf_op jit(solution)/shard_map/jit(_take)/gather | solution.py:48
  1.5 3.2 %fusion.36 = (s32[64]{0:T(128)S(1)}, s32[64]{0:T(128)S(1)}) fusion(s32[64]{0:T(128)} %param.14, s32[]{:T(128)} %bitcast.3, s32[]{:T(128)} %bitcast.4, s32[]{:T(128)} %bitcast.5, s32[]{:T(128)} %bitcast.6, s32[64]{0:T(128)} %param.13), kind=kLoop, calls=%fused_computation.59 | loop fusion | flops 1024 | bytes 1040 | tf_op jit(solution)/shard_map/jit(clip)/min | solution.py:48
  4.7 0.0 copy-done
  4.7 0.8 %gather_fusion = bf16[64,4096]{1,0:T(8,128)(2,1)S(1)} fusion(bf16[4,4096]{1,0:T(4,128)(2,1)S(1)} %copy-done, s32[1024]{0:T(1024)S(1)} %pad_clamp_fusion), kind=kCustom, calls=%fused_computation | custom fusion | bytes 1048832 | tf_op jit(solution)/shard_map/jit(_take)/gather | solution.py:43
  5.5 0.1 copy.34
  5.6 0.7 compare_and_fusion
  6.3 0.1 iota_compare_fusion
  6.3 7.0 %fusion.41 = (f32[64,4,8]{2,1,0:T(4,128)S(1)}, f32[64,4,8,128]{3,2,1,0:T(8,128)S(1)}) fusion(bf16[64,4,8,128]{3,2,1,0:T(8,128)(2,1)S(1)} %bitcast.106, pred[64]{0:T(512)(128)(4,1)S(1)} %compare_and_fusion, pred[64,128]{1,0:T(8,128)(4,1)S(1)} %iota_compare_fusion, bf16[64,128,512]{2,1,0:T(8,128)(2,1)} %param.10), kind=kOutput, calls=%fused_computation.63 | convolution fusion | flops 68155392 | bytes 9977920 | tf_op jit(solution)/shard_map/sgjd,stgd->sgjt/dot_general | solution.py:46
  13.4 0.1 copy.25
  13.5 0.0 copy-done.1
  13.5 0.1 select_reduce_fusion
  13.6 0.1 all_gather_reshape.3
  13.7 14.5 %all_gather.15 = f32[8,4,32]{2,1,0:T(4,128)S(1)} all-gather(f32[1,4,32]{2,1,0:T(4,128)S(1)} %all_gather_reshape.3), channel_id=1, replica_groups=mesh['rep'=2,'seq'=4,'head'=2,'sub'=2] {'seq','sub'}, dimensions={0}, use_global_device_ids=true | all-gather | bytes 4608 | tf_op jit(solution)/shard_map/all_gather | solution.py:12
  28.2 0.7 gather_fusion.1
  28.8 0.1 copy.28
  28.9 0.8 convert_reduce_fusion
  29.7 0.1 copy.26
  29.8 0.1 convolution_bitcast_fusion.1
  29.9 12.8 %all-gather.2 = f32[8,4,32]{2,1,0:T(4,128)S(1)} all-gather(f32[1,4,32]{2,1,0:T(4,128)S(1)} %convolution_bitcast_fusion.1), channel_id=2, replica_groups=mesh['rep'=2,'seq'=4,'head'=2,'sub'=2] {'seq','sub'}, dimensions={0}, use_global_device_ids=true | all-gather | bytes 4608 | tf_op jit(solution)/shard_map/all_gather | solution.py:12
  42.7 0.1 subtract_exponential_fusion.1
  42.8 4.7 %fusion.12 = f32[64,4,8,128]{3,2,1,0:T(8,128)S(1)} fusion(f32[64,4,8]{2,1,0:T(4,128)S(1)} %subtract_exponential_fusion.1, f32[64,4,8,128]{3,2,1,0:T(8,128)S(1)} %get-tuple-element.211, f32[64,4,8]{2,1,0:T(4,128)S(1)} %get-tuple-element.210, bf16[64,128,512]{2,1,0:T(8,128)(2,1)} %param.11), kind=kOutput, calls=%fused_computation.21 | convolution fusion | flops 67895296 | bytes 10502144 | tf_op jit(solution)/shard_map/sgjt,stgd->sgjd/dot_general | solution.py:55
  47.6 1.0 %convolution_bitcast_fusion = f32[1,4,4096]{2,1,0:T(4,128)S(1)} fusion(f32[8,8,32,128]{3,2,1,0:T(8,128)S(1)} %bitcast.108, s32[64]{0:T(128)S(1)} %copy-done.1), kind=kOutput, calls=%fused_computation.19 | convolution fusion | flops 12583168 | bytes 1114368 | tf_op jit(solution)/shard_map/dot_general | solution.py:67
  48.6 14.9 %all-gather.3 = f32[8,4,4096]{2,1,0:T(4,128)S(1)} all-gather(f32[1,4,4096]{2,1,0:T(4,128)S(1)} %convolution_bitcast_fusion), channel_id=3, replica_groups=mesh['rep'=2,'seq'=4,'head'=2,'sub'=2] {'seq','sub'}, dimensions={0}, use_global_device_ids=true | all-gather | bytes 589824 | tf_op jit(solution)/shard_map/all_gather | solution.py:12
  63.5 1.9 %while.19 = (s32[]{:T(128)}, f32[4,32]{1,0:T(4,128)S(1)}, f32[4,32]{1,0:T(4,128)S(1)}, f32[4,4096]{1,0:T(4,128)S(1)}, f32[8,4,32]{2,1,0:T(4,128)S(1)}, /*index=5...) while((s32[]{:T(128)}, f32[4,32]{1,0:T(4,128)S(1)}, ...), condition=%wide.region_4.5_spmd, body=%wide.region_3.4_spmd.sunk | while | flops 49925 | bytes 464023 | solution.py:17
  63.6 0.1 broadcast_bitcast_fusion.4
  63.7 0.1 fusion.48
  63.8 0.1 broadcast_bitcast_fusion.4
  63.9 0.1 fusion.48
  64.1 0.1 broadcast_bitcast_fusion.4
  64.2 0.1 fusion.48
  64.4 0.1 broadcast_bitcast_fusion.4
  64.5 0.1 fusion.48
  64.6 0.1 broadcast_bitcast_fusion.4
  64.7 0.1 fusion.48
  64.9 0.1 broadcast_bitcast_fusion.4
  65.0 0.1 fusion.48
  65.2 0.1 broadcast_bitcast_fusion.4
  65.3 0.1 fusion.48
  65.4 0.1 broadcast_bitcast_fusion.2
  65.5 4.6 %fusion.24 = f32[4,1024]{1,0:T(4,128)S(1)} fusion(bf16[4096,1024]{1,0:T(8,128)(2,1)} %param.15, f32[4,4096]{1,0:T(4,128)S(1)} %get-tuple-element.182, f32[1,4,32,128]{3,2,1,0:T(8,128)S(1)} %broadcast_bitcast_fusion.2), kind=kOutput, calls=%fused_computation.36 | convolution fusion | flops 33587200 | bytes 8536064 | tf_op jit(solution)/shard_map/dot_general | solution.py:76
  70.1 8.7 %psum.7 = bf16[4,1024]{1,0:T(4,128)(2,1)} all-reduce(f32[4,1024]{1,0:T(4,128)S(1)} %fusion.24), channel_id=1, replica_groups=mesh['rep'=2,'seq'=4,'head'=2,'sub'=2] {'head'}, use_global_device_ids=true, to_apply=%region_5.6 | all-reduce | flops 4096 | bytes 24576 | tf_op jit(solution)/shard_map/psum | solution.py:77
  (13 shorter events, 0.2 us)
Async XLA Ops:
  0.0 4.7 %copy-start = (bf16[4,4096]{1,0:T(4,128)(2,1)S(1)}, bf16[4,4096]{1,0:T(4,128)(2,1)}, u32[]{:S(2)}) copy-start(bf16[4,4096]{1,0:T(4,128)(2,1)} %param.9) | copy-start | bytes 98308
  0.0 13.5 %copy-start.1 = (s32[64]{0:T(128)S(1)}, s32[64]{0:T(128)}, u32[]{:S(2)}) copy-start(s32[64]{0:T(128)} %param.13) | copy-start | bytes 772
where the time goes:
time: 79.1 us; the launch traced here: 78.8 us
  blocking collectives  50.9 us (64%)
  matrix products  17.5 us (22%)
  other arithmetic  6.07 us (8%)
  local copies, waits for them, and re-layouts  4.05 us (5%)
    all_gather x3, blocking collectives, merged(): gathered = jax.tree.map(lambda a: lax.all_gather(a, axis), part)  42.2 us
    psum x1, blocking collectives, on_device(): return lax.psum(partial_out, 'head').astype(jnp.bfloat16)  8.73 us
    dot_general x1, matrix products, on_device(): jnp.einsum('sgjd,stgd->sgjt', picked, key_tiles, preferred_element_type=j...  7.04 us
    dot_general x1, matrix products, on_device(): jnp.einsum('sgjt,stgd->sgjd', probs, value_tiles, preferred_element_type=...  4.72 us
    dot_general x1, matrix products, on_device(): jnp.dot(attention, out_weight, preferred_element_type=jnp.float32)  4.59 us
    min x1, other arithmetic, on_device(): jnp.clip(jnp.take(seq_lengths, slot_owner, axis=0) - slot_page * PAGE, 0,...  3.19 us

commit v1 on v0

--- a/solution.py
+++ b/solution.py
@@ -74,7 +74,7 @@
     top_all, mass_all, out_all = merged((seq_peak, seq_mass, seq_out), ("seq", "sub"), merge_states)
     attention = spread(out_all, 1.0 / mass_all).astype(jnp.bfloat16)
     partial_out = jnp.dot(attention, out_weight, preferred_element_type=jnp.float32)
-    return lax.psum(partial_out, "head").astype(jnp.bfloat16)
+    return jnp.sum(lax.all_gather(partial_out, "head"), axis=0).astype(jnp.bfloat16)
 
 
 def solution(mesh):

time: 79.1 us -> 75.4 us (0.953)
  blocking collectives: 50.9 us -> 46.6 us
    psum x1 -> x0, blocking collectives: 8.73 us -> none  [on_device(): return lax.psum(partial_out, 'head').astype(jnp.bfloat16)]
    all_gather x0 -> x1, blocking collectives: none -> 4.4 us  [on_device(): lax.all_gather(partial_out, 'head')]
where the time goes in v1:
time: 75.4 us; the launch traced here: 75.1 us
  blocking collectives  46.6 us (62%)
  matrix products  17.5 us (23%)
  other arithmetic  6.68 us (9%)
  local copies, waits for them, and re-layouts  4.05 us (5%)
    all_gather x3, blocking collectives, merged(): gathered = jax.tree.map(lambda a: lax.all_gather(a, axis), part)  42.2 us
    dot_general x1, matrix products, on_device(): jnp.einsum('sgjd,stgd->sgjt', picked, key_tiles, preferred_element_type=j...  7.04 us
    dot_general x1, matrix products, on_device(): jnp.einsum('sgjt,stgd->sgjd', probs, value_tiles, preferred_element_type=...  4.72 us
    dot_general x1, matrix products, on_device(): jnp.dot(attention, out_weight, preferred_element_type=jnp.float32)  4.59 us
    all_gather x1, blocking collectives, on_device(): lax.all_gather(partial_out, 'head')  4.4 us
    min x1, other arithmetic, on_device(): jnp.clip(jnp.take(seq_lengths, slot_owner, axis=0) - slot_page * PAGE, 0,...  3.19 us

profile of v1, /device:TPU:0, one launch (start us, length us, event | category | flops | bytes accessed | tf_op | source)
XLA Modules:
  0.0 75.1 jit_solution(5350461292194375600)
XLA Ops:
  0.0 0.0 copy-start
  0.0 0.0 copy-start.1
  0.0 1.5 %fusion.39 = (s32[1]{0:T(128)}, s32[1]{0:T(128)}, s32[1]{0:T(128)}, s32[1]{0:T(128)}) fusion(s32[4]{0:T(128)} %param.12), kind=kLoop, calls=%fused_computation.62 | loop fusion | bytes 32 | tf_op jit(solution)/shard_map/jit(_take)/gather | solution.py:48
  1.5 3.2 %fusion.35 = (s32[64]{0:T(128)S(1)}, s32[64]{0:T(128)S(1)}) fusion(s32[64]{0:T(128)} %param.14, s32[]{:T(128)} %bitcast.3, s32[]{:T(128)} %bitcast.4, s32[]{:T(128)} %bitcast.5, s32[]{:T(128)} %bitcast.6, s32[64]{0:T(128)} %param.13), kind=kLoop, calls=%fused_computation.59 | loop fusion | flops 1024 | bytes 1040 | tf_op jit(solution)/shard_map/jit(clip)/min | solution.py:48
  4.7 0.0 copy-done
  4.7 0.8 %gather_fusion = bf16[64,4096]{1,0:T(8,128)(2,1)S(1)} fusion(bf16[4,4096]{1,0:T(4,128)(2,1)S(1)} %copy-done, s32[1024]{0:T(1024)S(1)} %pad_clamp_fusion), kind=kCustom, calls=%fused_computation | custom fusion | bytes 1048832 | tf_op jit(solution)/shard_map/jit(_take)/gather | solution.py:43
  5.5 0.1 copy.34
  5.6 0.7 compare_and_fusion
  6.3 0.1 iota_compare_fusion
  6.3 7.0 %fusion.40 = (f32[64,4,8]{2,1,0:T(4,128)S(1)}, f32[64,4,8,128]{3,2,1,0:T(8,128)S(1)}) fusion(bf16[64,4,8,128]{3,2,1,0:T(8,128)(2,1)S(1)} %bitcast.108, pred[64]{0:T(512)(128)(4,1)S(1)} %compare_and_fusion, pred[64,128]{1,0:T(8,128)(4,1)S(1)} %iota_compare_fusion, bf16[64,128,512]{2,1,0:T(8,128)(2,1)} %param.10), kind=kOutput, calls=%fused_computation.63 | convolution fusion | flops 68155392 | bytes 9977920 | tf_op jit(solution)/shard_map/sgjd,stgd->sgjt/dot_general | solution.py:46
  13.4 0.1 copy.25
  13.5 0.0 copy-done.1
  13.5 0.1 select_reduce_fusion
  13.6 0.1 all_gather_reshape.3
  13.7 14.5 %all_gather.21 = f32[8,4,32]{2,1,0:T(4,128)S(1)} all-gather(f32[1,4,32]{2,1,0:T(4,128)S(1)} %all_gather_reshape.3), channel_id=1, replica_groups=mesh['rep'=2,'seq'=4,'head'=2,'sub'=2] {'seq','sub'}, dimensions={0}, use_global_device_ids=true | all-gather | bytes 4608 | tf_op jit(solution)/shard_map/all_gather | solution.py:12
  28.2 0.7 gather_fusion.1
  28.8 0.1 copy.28
  28.9 0.8 %convert_reduce_fusion = f32[64,4,8]{2,1,0:T(4,128)S(1)} fusion(f32[64,4,8,128]{3,2,1,0:T(8,128)S(1)} %get-tuple-element.211, f32[64,4,8]{2,1,0:T(4,128)S(1)} %get-tuple-element.210), kind=kLoop, calls=%fused_computation.27 | loop fusion | flops 1046528 | bytes 1064960 | tf_op jit(solution)/shard_map/reduce_sum | solution.py:54
  29.7 0.1 copy.26
  29.8 0.1 convolution_bitcast_fusion.2
  29.9 12.8 %all-gather.3 = f32[8,4,32]{2,1,0:T(4,128)S(1)} all-gather(f32[1,4,32]{2,1,0:T(4,128)S(1)} %convolution_bitcast_fusion.2), channel_id=2, replica_groups=mesh['rep'=2,'seq'=4,'head'=2,'sub'=2] {'seq','sub'}, dimensions={0}, use_global_device_ids=true | all-gather | bytes 4608 | tf_op jit(solution)/shard_map/all_gather | solution.py:12
  42.7 0.1 subtract_exponential_fusion.1
  42.8 4.7 %fusion.12 = f32[64,4,8,128]{3,2,1,0:T(8,128)S(1)} fusion(f32[64,4,8]{2,1,0:T(4,128)S(1)} %subtract_exponential_fusion.1, f32[64,4,8,128]{3,2,1,0:T(8,128)S(1)} %get-tuple-element.211, f32[64,4,8]{2,1,0:T(4,128)S(1)} %get-tuple-element.210, bf16[64,128,512]{2,1,0:T(8,128)(2,1)} %param.11), kind=kOutput, calls=%fused_computation.21 | convolution fusion | flops 67895296 | bytes 10502144 | tf_op jit(solution)/shard_map/sgjt,stgd->sgjd/dot_general | solution.py:55
  47.6 1.0 %convolution_bitcast_fusion = f32[1,4,4096]{2,1,0:T(4,128)S(1)} fusion(f32[8,8,32,128]{3,2,1,0:T(8,128)S(1)} %bitcast.110, s32[64]{0:T(128)S(1)} %copy-done.1), kind=kOutput, calls=%fused_computation.19 | convolution fusion | flops 12583168 | bytes 1114368 | tf_op jit(solution)/shard_map/dot_general | solution.py:67
  48.6 14.9 %all-gather.4 = f32[8,4,4096]{2,1,0:T(4,128)S(1)} all-gather(f32[1,4,4096]{2,1,0:T(4,128)S(1)} %convolution_bitcast_fusion), channel_id=3, replica_groups=mesh['rep'=2,'seq'=4,'head'=2,'sub'=2] {'seq','sub'}, dimensions={0}, use_global_device_ids=true | all-gather | bytes 589824 | tf_op jit(solution)/shard_map/all_gather | solution.py:12
  63.5 1.9 %while.19 = (s32[]{:T(128)}, f32[4,32]{1,0:T(4,128)S(1)}, f32[4,32]{1,0:T(4,128)S(1)}, f32[4,4096]{1,0:T(4,128)S(1)}, f32[8,4,32]{2,1,0:T(4,128)S(1)}, /*index=5...) while((s32[]{:T(128)}, f32[4,32]{1,0:T(4,128)S(1)}, ...), condition=%wide.region_4.5_spmd, body=%wide.region_3.4_spmd.sunk | while | flops 49925 | bytes 464023 | solution.py:17
  63.6 0.1 broadcast_bitcast_fusion.4
  63.7 0.1 fusion.47
  63.8 0.1 broadcast_bitcast_fusion.4
  63.9 0.1 fusion.47
  64.1 0.1 broadcast_bitcast_fusion.4
  64.2 0.1 fusion.47
  64.4 0.1 broadcast_bitcast_fusion.4
  64.5 0.1 fusion.47
  64.6 0.1 broadcast_bitcast_fusion.4
  64.7 0.1 fusion.47
  64.9 0.1 broadcast_bitcast_fusion.4
  65.0 0.1 fusion.47
  65.2 0.1 broadcast_bitcast_fusion.4
  65.3 0.1 fusion.47
  65.4 0.1 broadcast_bitcast_fusion.2
  65.5 4.6 %convolution_bitcast_fusion.1 = f32[1,4,1024]{2,1,0:T(4,128)S(1)} fusion(bf16[4096,1024]{1,0:T(8,128)(2,1)} %param.15, f32[4,4096]{1,0:T(4,128)S(1)} %get-tuple-element.182, f32[1,4,32,128]{3,2,1,0:T(8,128)S(1)} %broadcast_bitcast_fusion.2), kind=kOutput, calls=%fused_computation.23 | convolution fusion | flops 33587200 | bytes 8536064 | tf_op jit(solution)/shard_map/dot_general | solution.py:76
  70.1 4.4 %all-gather.5 = f32[2,4,1024]{2,1,0:T(4,128)S(1)} all-gather(f32[1,4,1024]{2,1,0:T(4,128)S(1)} %convolution_bitcast_fusion.1), channel_id=4, replica_groups=mesh['rep'=2,'seq'=4,'head'=2,'sub'=2] {'head'}, dimensions={0}, use_global_device_ids=true | all-gather | bytes 49152 | tf_op jit(solution)/shard_map/all_gather | solution.py:77
  74.5 0.6 reduce_sum.22
  (13 shorter events, 0.2 us)
Async XLA Ops:
  0.0 4.7 %copy-start = (bf16[4,4096]{1,0:T(4,128)(2,1)S(1)}, bf16[4,4096]{1,0:T(4,128)(2,1)}, u32[]{:S(2)}) copy-start(bf16[4,4096]{1,0:T(4,128)(2,1)} %param.9) | copy-start | bytes 98308
  0.0 13.5 %copy-start.1 = (s32[64]{0:T(128)S(1)}, s32[64]{0:T(128)}, u32[]{:S(2)}) copy-start(s32[64]{0:T(128)} %param.13) | copy-start | bytes 772
